TPU v7x, 32 devices: a whole 2x2x4 slice. The times are simulated.
32 devices in a mesh: pop: 8 (over z, y), mp: 4 (over x, core).
Axes of the slice: x: 2, y: 2, z: 4, core: 2. Of those that a mesh axis runs over, the one named last changes fastest.
Arguments:
- token_ids: int32 [96, 4, 16], P('pop'), may hold values from 0 to 255
- fitness_ranks: int32 [96], P('pop'), may hold values from 0 to 143, as said below
- embedding: bfloat16 [256, 4096], P(None, 'mp'), may hold values from -6 to 6
- mix_weights: bfloat16 [2, 4096, 4096], P(None, 'mp'), may hold values from -0.09375 to 0.09375
- factors_in: bfloat16 [2, 96, 4, 4096], P(None, 'pop', None, 'mp'), may hold values from -6 to 6
- factors_out: bfloat16 [2, 96, 4, 4096], P(None, 'pop'), may hold values from -6 to 6
- decay_rates: float32 [2, 4096], P(None, 'mp'), may hold values from 0.2 to 0.98
- norm_gain: float32 [2, 4096], P(None, 'mp'), may hold values from 0.1 to 1.9
- reward_dir: float32 [4096], P('mp'), may hold values from -6 to 6
Outputs:
- final_features: bfloat16 [96, 4, 4096], P('pop', None, 'mp')
- scores: float32 [96, 4], P('pop')
- weight_step: float32 [2, 4096, 4096], P(None, 'mp', 'pop')
Inputs may be any that keep to these rules, and one draw needn't show every extreme that they name: `fitness_ranks`: ranks may repeat.
All inputs are finite; a program needn't handle non-finite values.
Results may differ from a plain program's by a relative error of at most 0.023.
Values may be sent and summed in bfloat16 or wider, within the bound.
A program may use at most 128 MiB of HBM per device.

v0:
```python
import jax
import jax.numpy as jnp
from jax import lax
from jax.sharding import PartitionSpec as P

noise_scale = 0.25
norm_eps = 1e-06
spread_eps = 1e-05


def recurrence(inputs, decay):
    carried = jnp.zeros(inputs.shape[1:], jnp.float32)
    states = []
    for step in range(inputs.shape[0]):
        carried = decay * carried + (1.0 - decay) * inputs[step]
        states.append(carried)
    return jnp.stack(states, axis=0)


def mixed_inputs(hidden, weight_rows):
    flat = hidden.reshape(-1, hidden.shape[-1])
    partial_value = jnp.dot(flat, weight_rows, preferred_element_type=jnp.float32)
    summed = lax.psum_scatter(
        partial_value.astype(jnp.bfloat16), "mp", scatter_dimension=1, tiled=True
    ).astype(jnp.float32)
    return summed


def project_rank(hidden, factor_rows):
    return jnp.einsum("tmsd,mrd->tmsr", hidden, factor_rows, preferred_element_type=jnp.float32)


def shards(
    token_ids,
    fitness_ranks,
    embedding,
    mix_weights,
    factors_in,
    factors_out,
    decay_rates,
    norm_gain,
    reward_dir,
):
    members, seq_count, step_count = token_ids.shape
    local_width = embedding.shape[1]
    vocab_size = embedding.shape[0]
    layers = mix_weights.shape[0]
    full_width = mix_weights.shape[2]
    rank_count = factors_in.shape[2]
    pop_count = lax.axis_size("pop")
    members_all = members * pop_count
    coef = noise_scale * (full_width * rank_count) ** (-0.5)
    position = lax.axis_index("mp")
    outputs_local = lax.dynamic_slice_in_dim(
        factors_out, position * local_width, local_width, 3
    ).astype(jnp.float32)
    onehot = (
        jnp.moveaxis(token_ids, 2, 0).reshape(-1)[:, None]
        == jnp.arange(vocab_size, dtype=jnp.int32)[None, :]
    ).astype(jnp.bfloat16)
    hidden = jnp.dot(onehot, embedding, preferred_element_type=jnp.float32).astype(jnp.bfloat16)
    hidden = hidden.reshape(step_count, members, seq_count, local_width)
    for layer_idx in range(layers):
        if layer_idx == 0:
            table = mixed_inputs(embedding, mix_weights[0])
            top = table.astype(jnp.bfloat16)
            rest = (table - top.astype(jnp.float32)).astype(jnp.bfloat16)
            base_mix = jnp.dot(onehot, top, preferred_element_type=jnp.float32) + jnp.dot(
                onehot, rest, preferred_element_type=jnp.float32
            )
        else:
            base_mix = mixed_inputs(hidden, mix_weights[layer_idx])
        base_mix = base_mix.reshape(hidden.shape)
        low_rank = lax.psum(project_rank(hidden, factors_in[layer_idx]), "mp")
        correction = jnp.einsum(
            "tmsr,mrd->tmsd", low_rank, outputs_local[layer_idx], precision=lax.Precision.HIGHEST
        )
        states = recurrence(base_mix + coef * correction, decay_rates[layer_idx])
        squares = lax.psum(jnp.sum(states * states, axis=3), "mp")
        norm_scale = lax.rsqrt(squares / full_width + norm_eps)
        hidden = (
            hidden.astype(jnp.float32) + states * norm_scale[..., None] * norm_gain[layer_idx]
        ).astype(jnp.bfloat16)
    dots_local = jnp.einsum(
        "tmsd,d->tms", hidden.astype(jnp.float32), reward_dir, precision=lax.Precision.HIGHEST
    )
    reward_terms = lax.psum(dots_local, "mp")
    final_features = hidden[step_count - 1]
    scores = jnp.mean(reward_terms, axis=0) * full_width ** (-0.5)
    ranks_every = lax.all_gather(fitness_ranks, "pop", axis=0, tiled=True)
    shares_all = ranks_every.astype(jnp.float32) / members_all
    rank_mean = jnp.mean(shares_all)
    rank_spread = jnp.mean((shares_all - rank_mean) * (shares_all - rank_mean)) + spread_eps
    shaped_all = (shares_all - rank_mean) * lax.rsqrt(rank_spread)
    columns = lax.all_to_all(factors_out, "pop", split_axis=3, concat_axis=1, tiled=True)
    weighted = (
        lax.all_gather(factors_in, "pop", axis=1, tiled=True).astype(jnp.float32)
        * shaped_all[None, :, None, None]
    ).astype(jnp.bfloat16)
    weight_delta = jnp.einsum(
        "lmri,lmro->lio", weighted, columns, preferred_element_type=jnp.float32
    )
    weight_step = weight_delta * (members_all * rank_count) ** (-0.5)
    return (final_features, scores, weight_step)


def solution(mesh):
    return jax.shard_map(
        shards,
        mesh=mesh,
        in_specs=(
            P("pop", None, None),
            P("pop"),
            P(None, "mp"),
            P(None, "mp", None),
            P(None, "pop", None, "mp"),
            P(None, "pop", None, None),
            P(None, "mp"),
            P(None, "mp"),
            P("mp"),
        ),
        out_specs=(P("pop", None, "mp"), P("pop", None), P(None, "mp", "pop")),
        check_vma=False,
    )
```

profile of v0, /device:TPU:0, one launch (start us, length us, event | category | flops | bytes accessed | tf_op | source)
XLA Modules:
  0.0 303.1 jit_solution(9531522630871206582)
XLA Ops:
  9.0 7.0 %fusion.9 = bf16[256,4096]{1,0:T(8,128)(2,1)} fusion(bf16[256,1024]{1,0:T(8,128)(2,1)S(1)} %copy-done, bf16[2,1024,4096]{2,1,0:T(8,128)(2,1)} %param.12), kind=kOutput, calls=%fused_computation.7 | convolution fusion | flops 2148532224 | bytes 11010048 | tf_op jit(solution)/shard_map/dot_general | solution.py:22
  19.8 3.4 %fusion.23 = f32[16,12,4,4]{0,3,2,1:T(4,128)S(1)} fusion(bf16[16,12,4,1024]{3,2,1,0:T(4,128)(2,1)} %reshape.39, bf16[2,12,4,1024]{3,2,1,0:T(4,128)(2,1)S(1)} %copy-done.8), kind=kOutput, calls=%fused_computation.32 | convolution fusion | flops 6291456 | bytes 1683456 | tf_op jit(solution)/shard_map/tmsd,mrd->tmsr/dot_general | solution.py:30
  23.1 14.2 %psum.35 = f32[16,12,4,4]{0,3,2,1:T(4,128)S(1)} all-reduce(f32[16,12,4,4]{0,3,2,1:T(4,128)S(1)} %fusion.23), channel_id=1, replica_groups=mesh['pop'=8,'mp'=4] {'mp'}, use_global_device_ids=true, to_apply=%region_1.0 | all-reduce | flops 3072 | bytes 24576 | tf_op jit(solution)/shard_map/psum | solution.py:74
  37.4 3.1 %convolution_multiply_fusion.1 = f32[12,1024,16,4]{1,2,3,0:T(8,128)} fusion(f32[16,12,4,4]{0,3,2,1:T(4,128)S(1)} %psum.35, bf16[2,12,4,4096]{3,2,1,0:T(4,128)(2,1)S(1)} %copy-done.7, s32[]{:T(128)S(6)} %select_n.3), kind=kOutput, calls=%fused_computation.21 | convolution fusion | flops 38535168 | bytes 3342340 | tf_op jit(solution)/shard_map/tmsr,mrd->tmsd/dot_general | solution.py:75
  40.5 9.7 %reduce-scatter.3.cloned.1.call-done = bf16[256,1024]{1,0:T(8,128)(2,1)} async-done(((bf16[256,4096]{1,0:T(8,128)(2,1)}), bf16[256,1024]{1,0:T(8,128)(2,1)}) %reduce-scatter.3.cloned.1.call-update) | async-done | bytes 524304 | tf_op jit(solution)/shard_map/reduce_scatter | solution.py:23
  54.2 4.8 %reshape.40 = f32[16,12,4,1024]{3,2,1,0:T(4,128)} reshape(f32[768,1024]{1,0:T(8,128)} %convolution_add_fusion) | data formatting | bytes 6291456 | tf_op jit(solution)/shard_map/reshape | solution.py:73
  59.0 5.3 %fusion.13 = f32[16,12,4,1024]{3,2,1,0:T(4,128)S(1)} fusion(f32[16,12,4,1024]{3,2,1,0:T(4,128)} %reshape.40, f32[12,1024,16,4]{1,2,3,0:T(8,128)} %convolution_multiply_fusion.1), kind=kLoop, calls=%fused_computation.12 | loop fusion | flops 786432 | bytes 9437184 | tf_op jit(solution)/shard_map/add | solution.py:78
  90.4 4.9 %stack.7 = f32[768,1024]{1,0:T(8,128)} reshape(f32[16,12,4,1024]{3,2,1,0:T(4,128)} %fusion.52) | data formatting | bytes 6291456 | tf_op jit(solution)/shard_map/stack | solution.py:17
  98.1 10.7 %psum.36 = f32[16,12,4]{0,2,1:T(4,128)S(1)} all-reduce(f32[16,12,4]{0,2,1:T(4,128)S(1)} %copy.84), channel_id=1, replica_groups=mesh['pop'=8,'mp'=4] {'mp'}, use_global_device_ids=true, to_apply=%region_3.0 | all-reduce | flops 768 | bytes 6144 | tf_op jit(solution)/shard_map/psum | solution.py:79
  109.0 12.7 %fusion.6 = bf16[768,4096]{1,0:T(8,128)(2,1)} fusion(bf16[2,1024,4096]{2,1,0:T(8,128)(2,1)} %param.12, f32[768,1024]{1,0:T(8,128)} %stack.7, bf16[768,1024]{1,0:T(8,128)(2,1)S(1)} %convolution_convert_fusion, f32[1024]{0:T(1024)S(1)} %bitcast.112, f32[768]{0:T(1024)S(1)} %mul.1061), kind=kOutput, calls=%fused_computation.6 | convolution fusion | flops 6449528832 | bytes 19405824 | tf_op jit(solution)/shard_map/dot_general | solution.py:22
  121.8 9.1 %copy.71 = bf16[2,12,4,4096]{1,2,0,3:T(4,128)(2,1)} copy(bf16[2,12,4,4096]{3,2,1,0:T(4,128)(2,1)S(1)} %copy-done.7) | data formatting | bytes 1572864 | tf_op args[5]
  130.9 17.7 %reshape.57 = bf16[8,2,24576]{2,1,0:T(2,128)(2,1)} reshape(bf16[4096,2,4,12]{3,2,1,0:T(4,128)(2,1)} %bitcast.75) | data formatting | bytes 1572864
  148.6 5.7 %all-to-all-start = ((bf16[8,2,24576]{2,1,0:T(2,128)(2,1)}), bf16[8,2,24576]{2,1,0:T(2,128)(2,1)S(1)}, u32[]{:S(2)}, u32[]{:S(2)}) async-start(bf16[8,2,24576]{2,1,0:T(2,128)(2,1)} %reshape.57), calls=%async_computation.2 | async-start | bytes 1572864 | tf_op jit(solution)/shard_map/all_to_all | solution.py:95
  155.9 19.1 %all-reduce = s32[96]{0:T(128)S(1)} all-reduce(s32[96]{0:T(128)S(1)} %dynamic-update-slice), channel_id=1, replica_groups=mesh['pop'=8,'mp'=4] {'pop'}, use_global_device_ids=true, to_apply=%add | all-reduce | flops 96 | bytes 768
  177.5 20.4 %reshape.58 = bf16[4096,2,4,12]{3,2,1,0:T(4,128)(2,1)} reshape(bf16[8,2,24576]{2,1,0:T(2,128)(2,1)S(1)} %all-to-all-done) | data formatting | bytes 1572864
  197.9 12.0 %copy.72 = bf16[2,12,4,8,512]{4,2,1,3,0:T(4,128)(2,1)S(1)} copy(bf16[2,12,4,8,512]{1,2,0,4,3:T(4,128)(2,1)} %bitcast.74) | data formatting | bytes 1572864 | tf_op jit(solution)/shard_map/all_to_all | solution.py:95
  212.1 3.4 %bitcast_multiply_fusion = f32[2,1024,512]{2,1,0:T(8,128)} fusion(bf16[2,96,4,1024]{3,2,1,0:T(4,128)(2,1)S(1)} %multiply_convert_fusion, bf16[2,96,4,512]{3,2,1,0:T(4,128)(2,1)S(1)} %bitcast.76), kind=kOutput, calls=%fused_computation.8 | convolution fusion | flops 806354944 | bytes 6553600 | tf_op jit(solution)/shard_map/lmri,lmro->lio/dot_general | solution.py:100
  220.5 11.7 %psum.37 = f32[16,12,4,4]{0,3,2,1:T(4,128)S(1)} all-reduce(f32[16,12,4,4]{0,3,2,1:T(4,128)S(1)} %fusion.26), channel_id=1, replica_groups=mesh['pop'=8,'mp'=4] {'mp'}, use_global_device_ids=true, to_apply=%region_5.0 | all-reduce | flops 3072 | bytes 24576 | tf_op jit(solution)/shard_map/psum | solution.py:74
  232.2 3.1 %convolution_multiply_fusion = f32[12,1024,16,4]{1,2,3,0:T(8,128)} fusion(f32[16,12,4,4]{0,3,2,1:T(4,128)S(1)} %psum.37, bf16[2,12,4,4096]{3,2,1,0:T(4,128)(2,1)S(1)} %copy-done.7, s32[]{:T(128)S(6)} %add.456, s32[]{:T(128)S(6)} %select_n.3), kind=kOutput, calls=%fused_computation.20 | convolution fusion | flops 38535168 | bytes 3342344 | tf_op jit(solution)/shard_map/tmsr,mrd->tmsd/dot_general | solution.py:75
  235.3 4.1 %reshape.44 = f32[16,12,4,1024]{3,2,1,0:T(4,128)} reshape(bf16[768,1024]{1,0:T(8,128)(2,1)} %reduce-scatter.5.cloned.1.call-done) | data formatting | bytes 4718592 | tf_op jit(solution)/shard_map/reshape | solution.py:73
  239.4 5.3 %fusion.12 = f32[16,12,4,1024]{3,2,1,0:T(4,128)S(1)} fusion(f32[16,12,4,1024]{3,2,1,0:T(4,128)} %reshape.44, f32[12,1024,16,4]{1,2,3,0:T(8,128)} %convolution_multiply_fusion), kind=kLoop, calls=%fused_computation.10 | loop fusion | flops 786432 | bytes 9437184 | tf_op jit(solution)/shard_map/add | solution.py:78
  264.0 10.5 %psum.38 = f32[16,12,4]{0,2,1:T(4,128)S(1)} all-reduce(f32[16,12,4]{0,2,1:T(4,128)S(1)} %copy.85), channel_id=1, replica_groups=mesh['pop'=8,'mp'=4] {'mp'}, use_global_device_ids=true, to_apply=%region_7.0 | all-reduce | flops 768 | bytes 6144 | tf_op jit(solution)/shard_map/psum | solution.py:79
  278.5 5.6 %fusion.14 = f32[1,16,12,4]{1,0,3,2:T(1,128)S(1)} fusion(f32[1024,1,1,1]{0,1,3,2:T(1,128)S(1)} %bitcast.114, bf16[16,12,4,1024]{3,2,1,0:T(4,128)(2,1)S(1)} %add_convert_fusion), kind=kOutput, calls=%fused_computation.23 | convolution fusion | flops 9437184 | bytes 1580032 | tf_op jit(solution)/shard_map/tmsd,d->tms/dot_general | solution.py:84
  284.1 10.6 %psum.39 = f32[16,12,4]{0,2,1:T(4,128)S(1)} all-reduce(f32[16,12,4]{0,2,1:T(4,128)S(1)} %bitcast.110), channel_id=1, replica_groups=mesh['pop'=8,'mp'=4] {'mp'}, use_global_device_ids=true, to_apply=%region_8.0 | all-reduce | flops 768 | bytes 6144 | tf_op jit(solution)/shard_map/psum | solution.py:87
  (104 shorter events, 70.7 us)
Async XLA Ops:
  8.0 1.1 copy-start
  8.0 8.7 %copy-start.10 = (f32[2,1024]{1,0:T(2,128)S(1)}, f32[2,1024]{1,0:T(2,128)}, u32[]{:S(2)}) copy-start(f32[2,1024]{1,0:T(2,128)} %param.15) | copy-start | bytes 24580
  8.0 8.8 %copy-start.11 = (f32[2,1024]{1,0:T(2,128)S(1)}, f32[2,1024]{1,0:T(2,128)}, u32[]{:S(2)}) copy-start(f32[2,1024]{1,0:T(2,128)} %param.16) | copy-start | bytes 24580
  8.0 8.8 %copy-start.9 = (s32[12,4,16]{2,1,0:T(4,128)S(1)}, s32[12,4,16]{2,1,0:T(4,128)}, u32[]{:S(2)}) copy-start(s32[12,4,16]{2,1,0:T(4,128)} %param.9) | copy-start | bytes 9220
  8.0 42.1 %reduce-scatter.3.cloned.1.call-start = ((), (), s32[]{:S(2)}) async-start(), calls=%async_computation.3 | async-start | bytes 2621440 | tf_op jit(solution)/shard_map/reduce_scatter | solution.py:23
  16.1 3.6 %copy-start.8 = (bf16[2,12,4,1024]{3,2,1,0:T(4,128)(2,1)S(1)}, bf16[2,12,4,1024]{3,2,1,0:T(4,128)(2,1)}, u32[]{:S(2)}) copy-start(bf16[2,12,4,1024]{3,2,1,0:T(4,128)(2,1)} %param.13) | copy-start | bytes 589828
  16.1 193.8 %all-gather.2.cloned.1.call-start = ((), (), s32[]{:S(2)}) async-start(), calls=%async_computation.5 | async-start | bytes 1769472 | tf_op jit(solution)/shard_map/all_gather | solution.py:97
  16.7 218.6 %reduce-scatter.5.cloned.1.call-start = ((), (), s32[]{:S(2)}) async-start(), calls=%async_computation.4 | async-start | bytes 7864320 | tf_op jit(solution)/shard_map/reduce_scatter | solution.py:23
  17.7 19.6 %copy-start.7 = (bf16[2,12,4,4096]{3,2,1,0:T(4,128)(2,1)S(1)}, bf16[2,12,4,4096]{3,2,1,0:T(4,128)(2,1)}, u32[]{:S(2)}) copy-start(bf16[2,12,4,4096]{3,2,1,0:T(4,128)(2,1)} %param.14) | copy-start | bytes 2359300
  50.2 1.7 copy-start.6
  64.3 1.8 copy-start.2
  130.9 23.5 %copy-start.14 = (u32[32]{0:T(128)S(1)}, u32[32]{0:T(128)}, u32[]{:S(2)}) copy-start(u32[32]{0:T(128)} %constant.44) | copy-start | bytes 388
  130.9 24.7 %copy-start.13 = (s32[12]{0:T(128)S(1)}, s32[12]{0:T(128)}, u32[]{:S(2)}) copy-start(s32[12]{0:T(128)} %param.10) | copy-start | bytes 148
  148.6 28.9 %all-to-all-start = ((bf16[8,2,24576]{2,1,0:T(2,128)(2,1)}), bf16[8,2,24576]{2,1,0:T(2,128)(2,1)S(1)}, u32[]{:S(2)}, u32[]{:S(2)}) async-start(bf16[8,2,24576]{2,1,0:T(2,128)(2,1)} %reshape.57), calls=%async_computation.2 | async-start | bytes 1572864 | tf_op jit(solution)/shard_map/all_to_all | solution.py:95
  212.1 3.5 %copy-start.5 = (bf16[16,12,4,1024]{3,2,1,0:T(4,128)(2,1)S(1)}, bf16[16,12,4,1024]{3,2,1,0:T(4,128)(2,1)}, u32[]{:S(2)}) copy-start(bf16[16,12,4,1024]{3,2,1,0:T(4,128)(2,1)} %reshape.39) | copy-start | bytes 4718596
  244.7 1.7 copy-start.3
  261.5 1.7 copy-start.4
  274.7 20.7 %copy-start.1 = (bf16[256,1024]{1,0:T(8,128)(2,1)S(1)}, bf16[256,1024]{1,0:T(8,128)(2,1)}, u32[]{:S(2)}) copy-start(bf16[256,1024]{1,0:T(8,128)(2,1)} %param.11) | copy-start | bytes 1572868
  274.7 3.7 %copy-start.12 = (f32[1024]{0:T(1024)S(1)}, f32[1024]{0:T(1024)}, u32[]{:S(2)}) copy-start(f32[1024]{0:T(1024)} %param.17) | copy-start | bytes 12292
Sparse Core Ops, SparseCore 0:
  16.2 33.8 reduce-scatter.2
  121.9 58.4 reduce-scatter.4
Sparse Core Ops, SparseCore 1:
  18.8 46.8 all-gather.1
where the time goes:
time: 308 us; the launch traced here: 303 us
  local copies, waits for them, and re-layouts  82.4 us (27%)
  blocking collectives  76.8 us (25%)
  other arithmetic  64.7 us (21%)
  matrix products  45 us (15%)
  between operations  18.1 us (6%)
  waiting for transfers between devices  10.3 us (3%)
  starting transfers between devices  5.86 us (2%)
    unnamed x39, local copies, waits for them, and re-layouts  53.2 us
    unnamed x30, other arithmetic  38.4 us
    psum x2, blocking collectives, shards(): low_rank = lax.psum(project_rank(hidden, factors_in[layer_idx]), 'mp')  25.9 us
    psum x2, blocking collectives, shards(): squares = lax.psum(jnp.sum(states * states, axis=3), 'mp')  21.2 us
    dot_general x2, matrix products, mixed_inputs(): jnp.dot(flat, weight_rows, preferred_element_type=jnp.float32)  19.8 us
    unnamed x1, blocking collectives  19.1 us
    all_to_all x1, local copies, waits for them, and re-layouts, shards(): lax.all_to_all(factors_out, 'pop', split_axis=3, concat_axis=1, tiled=True)  12 us
    psum x1, blocking collectives, shards(): reward_terms = lax.psum(dots_local, 'mp')  10.6 us
  transfers between devices with their start and end apart: 4, of which 1 were waited for; matrix products, arithmetic and copies ran while one was open for 48% of the time, Pallas kernels for 0%

commit v1 on v0

--- a/solution.py
+++ b/solution.py
@@ -92,7 +92,10 @@
     rank_mean = jnp.mean(shares_all)
     rank_spread = jnp.mean((shares_all - rank_mean) * (shares_all - rank_mean)) + spread_eps
     shaped_all = (shares_all - rank_mean) * lax.rsqrt(rank_spread)
-    columns = lax.all_to_all(factors_out, "pop", split_axis=3, concat_axis=1, tiled=True)
+    size = lax.axis_size("pop")
+    pieces = jnp.stack(jnp.split(factors_out, size, axis=3), axis=0)
+    pieces = lax.all_to_all(pieces, "pop", split_axis=0, concat_axis=0)
+    columns = jnp.concatenate(pieces, axis=1)
     weighted = (
         lax.all_gather(factors_in, "pop", axis=1, tiled=True).astype(jnp.float32)
         * shaped_all[None, :, None, None]

time: 308 us -> 235 us (0.76); the launches traced: 303 us -> 234 us
  local copies, waits for them, and re-layouts: 82.4 us -> 33.5 us
  other arithmetic: 64.7 us -> 48.1 us
    unnamed x39 -> x45, local copies, waits for them, and re-layouts: 53.2 us -> 16.5 us
    unnamed x30, other arithmetic: 38.4 us -> 25.6 us
    all_to_all x1 -> x0, local copies, waits for them, and re-layouts: 12 us -> none  [shards(): lax.all_to_all(factors_out, 'pop', split_axis=3, concat_axis=1, tiled=True)]
  transfers between devices with their start and end apart: 4 -> 4, of which waited for: 1 -> 1; matrix products, arithmetic and copies ran while one was open for 48% -> 35% of each run, Pallas kernels for 0% -> 0%
where the time goes in v1:
time: 235 us; the launch traced here: 234 us
  blocking collectives  75.4 us (32%)
  other arithmetic  48.1 us (20%)
  matrix products  43.6 us (19%)
  local copies, waits for them, and re-layouts  33.5 us (14%)
  between operations  17.9 us (8%)
  waiting for transfers between devices  9.34 us (4%)
  starting transfers between devices  5.68 us (2%)
    psum x2, blocking collectives, shards(): low_rank = lax.psum(project_rank(hidden, factors_in[layer_idx]), 'mp')  25.8 us
    unnamed x30, other arithmetic  25.6 us
    psum x2, blocking collectives, shards(): squares = lax.psum(jnp.sum(states * states, axis=3), 'mp')  20.7 us
    dot_general x2, matrix products, mixed_inputs(): jnp.dot(flat, weight_rows, preferred_element_type=jnp.float32)  20 us
    unnamed x1, blocking collectives  18.7 us
    unnamed x45, local copies, waits for them, and re-layouts  16.5 us
    psum x1, blocking collectives, shards(): reward_terms = lax.psum(dots_local, 'mp')  10.3 us
    add x2, other arithmetic, shards(): states = recurrence(base_mix + coef * correction, decay_rates[layer_idx])  9.61 us
  transfers between devices with their start and end apart: 4, of which 1 were waited for; matrix products, arithmetic and copies ran while one was open for 35% of the time, Pallas kernels for 0%

profile of v1, /device:TPU:0, one launch (start us, length us, event | category | flops | bytes accessed | tf_op | source)
XLA Modules:
  0.0 233.5 jit_solution(15376411211532444951)
XLA Ops:
  9.0 7.0 %fusion.9 = bf16[256,4096]{1,0:T(8,128)(2,1)} fusion(bf16[256,1024]{1,0:T(8,128)(2,1)S(1)} %copy-done, bf16[2,1024,4096]{2,1,0:T(8,128)(2,1)} %param.12), kind=kOutput, calls=%fused_computation.7 | convolution fusion | flops 2148532224 | bytes 11010048 | tf_op jit(solution)/shard_map/dot_general | solution.py:22
  17.7 2.3 reshape.45
  20.0 3.4 %fusion.23 = f32[16,12,4,4]{0,3,2,1:T(4,128)S(1)} fusion(bf16[16,12,4,1024]{3,2,1,0:T(4,128)(2,1)} %reshape.45, bf16[2,12,4,1024]{3,2,1,0:T(4,128)(2,1)S(1)} %copy-done.9), kind=kOutput, calls=%fused_computation.32 | convolution fusion | flops 6291456 | bytes 1683456 | tf_op jit(solution)/shard_map/tmsd,mrd->tmsr/dot_general | solution.py:30
  23.3 14.0 %psum.35 = f32[16,12,4,4]{0,3,2,1:T(4,128)S(1)} all-reduce(f32[16,12,4,4]{0,3,2,1:T(4,128)S(1)} %fusion.23), channel_id=1, replica_groups=mesh['pop'=8,'mp'=4] {'mp'}, use_global_device_ids=true, to_apply=%region_1.0 | all-reduce | flops 3072 | bytes 24576 | tf_op jit(solution)/shard_map/psum | solution.py:74
  37.4 4.0 %convolution_multiply_fusion.1 = f32[12,1024,16,4]{1,2,3,0:T(8,128)} fusion(f32[16,12,4,4]{0,3,2,1:T(4,128)S(1)} %psum.35, bf16[2,12,4,4096]{3,2,1,0:T(4,128)(2,1)} %param.14, s32[]{:T(128)S(6)} %select_n.3), kind=kOutput, calls=%fused_computation.21 | convolution fusion | flops 38535168 | bytes 3256324 | tf_op jit(solution)/shard_map/tmsr,mrd->tmsd/dot_general | solution.py:75
  41.4 8.8 %reduce-scatter.3.cloned.1.call-done = bf16[256,1024]{1,0:T(8,128)(2,1)} async-done(((bf16[256,4096]{1,0:T(8,128)(2,1)}), bf16[256,1024]{1,0:T(8,128)(2,1)}) %reduce-scatter.3.cloned.1.call-update) | async-done | bytes 524304 | tf_op jit(solution)/shard_map/reduce_scatter | solution.py:23
  52.6 2.6 %reshape.46 = f32[16,12,4,1024]{3,2,1,0:T(4,128)} reshape(f32[768,1024]{1,0:T(8,128)S(1)} %convolution_add_fusion) | data formatting | bytes 6291456 | tf_op jit(solution)/shard_map/reshape | solution.py:73
  55.1 5.3 %fusion.13 = f32[16,12,4,1024]{3,2,1,0:T(4,128)S(1)} fusion(f32[16,12,4,1024]{3,2,1,0:T(4,128)} %reshape.46, f32[12,1024,16,4]{1,2,3,0:T(8,128)} %convolution_multiply_fusion.1), kind=kLoop, calls=%fused_computation.12 | loop fusion | flops 786432 | bytes 9437184 | tf_op jit(solution)/shard_map/add | solution.py:78
  77.2 2.7 %stack.25 = f32[768,1024]{1,0:T(8,128)} reshape(f32[16,12,4,1024]{3,2,1,0:T(4,128)S(1)} %fusion.52) | data formatting | bytes 6291456 | tf_op jit(solution)/shard_map/stack | solution.py:17
  80.7 10.5 %psum.36 = f32[16,12,4]{0,2,1:T(4,128)S(1)} all-reduce(f32[16,12,4]{0,2,1:T(4,128)S(1)} %copy.70), channel_id=1, replica_groups=mesh['pop'=8,'mp'=4] {'mp'}, use_global_device_ids=true, to_apply=%region_3.0 | all-reduce | flops 768 | bytes 6144 | tf_op jit(solution)/shard_map/psum | solution.py:79
  91.5 12.9 %fusion.6 = bf16[768,4096]{1,0:T(8,128)(2,1)} fusion(bf16[2,1024,4096]{2,1,0:T(8,128)(2,1)} %param.12, f32[768,1024]{1,0:T(8,128)} %stack.25, bf16[768,1024]{1,0:T(8,128)(2,1)} %copy-done.3, f32[1024]{0:T(1024)S(1)} %bitcast.122, f32[768]{0:T(1024)S(1)} %mul.1061), kind=kOutput, calls=%fused_computation.6 | convolution fusion | flops 6449528832 | bytes 19405824 | tf_op jit(solution)/shard_map/dot_general | solution.py:22
  117.1 5.6 %all-to-all-start = ((bf16[8,2,12,4,512]{4,3,2,1,0:T(4,128)(2,1)}), bf16[8,2,12,4,512]{4,3,2,1,0:T(4,128)(2,1)}, u32[]{:S(2)}, u32[]{:S(2)}) async-start(bf16[8,2,12,4,512]{4,3,2,1,0:T(4,128)(2,1)} %bitcast_dynamic-update-slice_fusion), calls=%async_computation.2 | async-start | bytes 1572864 | tf_op jit(solution)/shard_map/all_to_all | solution.py:97
  124.2 18.7 %all-reduce = s32[96]{0:T(128)S(1)} all-reduce(s32[96]{0:T(128)S(1)} %dynamic-update-slice), channel_id=1, replica_groups=mesh['pop'=8,'mp'=4] {'pop'}, use_global_device_ids=true, to_apply=%add | all-reduce | flops 96 | bytes 768
  145.4 2.3 %copy.58 = bf16[2,8,12,4,512]{4,3,2,1,0:T(4,128)(2,1)} copy(bf16[2,8,12,4,512]{4,3,2,0,1:T(4,128)(2,1)} %bitcast.37) | data formatting | bytes 1572864 | tf_op jit(solution)/shard_map/reshape | solution.py:98
  149.9 3.4 %bitcast_multiply_fusion = f32[2,1024,512]{2,1,0:T(8,128)} fusion(bf16[2,96,4,1024]{3,2,1,0:T(4,128)(2,1)S(1)} %multiply_convert_fusion, bf16[2,96,4,512]{3,2,1,0:T(4,128)(2,1)S(1)} %bitcast.86), kind=kOutput, calls=%fused_computation.8 | convolution fusion | flops 806354944 | bytes 6553600 | tf_op jit(solution)/shard_map/lmri,lmro->lio/dot_general | solution.py:103
  157.6 11.8 %psum.37 = f32[16,12,4,4]{0,3,2,1:T(4,128)S(1)} all-reduce(f32[16,12,4,4]{0,3,2,1:T(4,128)S(1)} %fusion.26), channel_id=1, replica_groups=mesh['pop'=8,'mp'=4] {'mp'}, use_global_device_ids=true, to_apply=%region_5.0 | all-reduce | flops 3072 | bytes 24576 | tf_op jit(solution)/shard_map/psum | solution.py:74
  169.4 2.3 %convolution_multiply_fusion = f32[12,1024,16,4]{1,2,3,0:T(8,128)S(1)} fusion(f32[16,12,4,4]{0,3,2,1:T(4,128)S(1)} %psum.37, bf16[2,12,4,4096]{3,2,1,0:T(4,128)(2,1)} %param.14, s32[]{:T(128)S(6)} %add.456, s32[]{:T(128)S(6)} %select_n.3), kind=kOutput, calls=%fused_computation.20 | convolution fusion | flops 38535168 | bytes 3256328 | tf_op jit(solution)/shard_map/tmsr,mrd->tmsd/dot_general | solution.py:75
  171.8 4.1 %reshape.52 = f32[16,12,4,1024]{3,2,1,0:T(4,128)} reshape(bf16[768,1024]{1,0:T(8,128)(2,1)} %reduce-scatter.5.cloned.1.call-done) | data formatting | bytes 4718592 | tf_op jit(solution)/shard_map/reshape | solution.py:73
  175.9 4.3 %fusion.12 = f32[16,12,4,1024]{3,2,1,0:T(4,128)S(1)} fusion(f32[16,12,4,1024]{3,2,1,0:T(4,128)} %reshape.52, f32[12,1024,16,4]{1,2,3,0:T(8,128)S(1)} %convolution_multiply_fusion), kind=kLoop, calls=%fused_computation.10 | loop fusion | flops 786432 | bytes 9437184 | tf_op jit(solution)/shard_map/add | solution.py:78
  192.5 2.6 %multiply_reduce_fusion = f32[16,12,4]{2,1,0:T(8,128)S(1)} fusion(f32[16,12,4,1024]{3,2,1,0:T(4,128)} %fusion.35), kind=kLoop, calls=%fused_computation.15 | loop fusion | flops 1572096 | bytes 3148800 | tf_op jit(solution)/shard_map/reduce_sum | solution.py:79
  195.2 10.3 %psum.38 = f32[16,12,4]{0,2,1:T(4,128)S(1)} all-reduce(f32[16,12,4]{0,2,1:T(4,128)S(1)} %copy.71), channel_id=1, replica_groups=mesh['pop'=8,'mp'=4] {'mp'}, use_global_device_ids=true, to_apply=%region_7.0 | all-reduce | flops 768 | bytes 6144 | tf_op jit(solution)/shard_map/psum | solution.py:79
  205.7 3.0 %add_convert_fusion = bf16[16,12,4,1024]{3,2,1,0:T(4,128)(2,1)S(1)} fusion(f32[16,12,4,1024]{3,2,1,0:T(4,128)} %fusion.35, bf16[16,12,4,1024]{3,2,1,0:T(4,128)(2,1)S(1)} %copy-done.6, f32[1024]{0:T(1024)S(1)} %bitcast.121, f32[16,12,4]{2,1,0:T(8,128)S(1)} %copy.57), kind=kLoop, calls=%fused_computation.14 | loop fusion | flops 3932160 | bytes 6298624 | tf_op jit(solution)/shard_map/convert_element_type | solution.py:83
  209.5 5.6 %fusion.14 = f32[1,16,12,4]{1,0,3,2:T(1,128)S(1)} fusion(f32[1024,1,1,1]{0,1,3,2:T(1,128)S(1)} %bitcast.124, bf16[16,12,4,1024]{3,2,1,0:T(4,128)(2,1)S(1)} %add_convert_fusion), kind=kOutput, calls=%fused_computation.23 | convolution fusion | flops 9437184 | bytes 1580032 | tf_op jit(solution)/shard_map/tmsd,d->tms/dot_general | solution.py:84
  215.0 10.3 %psum.39 = f32[16,12,4]{0,2,1:T(4,128)S(1)} all-reduce(f32[16,12,4]{0,2,1:T(4,128)S(1)} %bitcast.120), channel_id=1, replica_groups=mesh['pop'=8,'mp'=4] {'mp'}, use_global_device_ids=true, to_apply=%region_8.0 | all-reduce | flops 768 | bytes 6144 | tf_op jit(solution)/shard_map/psum | solution.py:87
  (111 shorter events, 58.0 us)
Async XLA Ops:
  8.0 1.1 copy-start
  8.0 8.7 %copy-start.10 = (s32[12,4,16]{2,1,0:T(4,128)S(1)}, s32[12,4,16]{2,1,0:T(4,128)}, u32[]{:S(2)}) copy-start(s32[12,4,16]{2,1,0:T(4,128)} %param.9) | copy-start | bytes 9220
  8.0 42.1 %reduce-scatter.3.cloned.1.call-start = ((), (), s32[]{:S(2)}) async-start(), calls=%async_computation.3 | async-start | bytes 2621440 | tf_op jit(solution)/shard_map/reduce_scatter | solution.py:23
  16.1 3.9 %copy-start.9 = (bf16[2,12,4,1024]{3,2,1,0:T(4,128)(2,1)S(1)}, bf16[2,12,4,1024]{3,2,1,0:T(4,128)(2,1)}, u32[]{:S(2)}) copy-start(bf16[2,12,4,1024]{3,2,1,0:T(4,128)(2,1)} %param.13) | copy-start | bytes 589828
  16.1 131.6 %all-gather.2.cloned.1.call-start = ((), (), s32[]{:S(2)}) async-start(), calls=%async_computation.5 | async-start | bytes 1769472 | tf_op jit(solution)/shard_map/all_gather | solution.py:100
  16.7 155.1 %reduce-scatter.5.cloned.1.call-start = ((), (), s32[]{:S(2)}) async-start(), calls=%async_computation.4 | async-start | bytes 7864320 | tf_op jit(solution)/shard_map/reduce_scatter | solution.py:23
  17.7 23.7 %copy-start.3 = (bf16[768,1024]{1,0:T(8,128)(2,1)}, bf16[768,1024]{1,0:T(8,128)(2,1)S(1)}, u32[]{:S(2)}) copy-start(bf16[768,1024]{1,0:T(8,128)(2,1)S(1)} %convolution_convert_fusion) | copy-start | bytes 4718596
  17.7 19.7 %copy-start.11 = (f32[2,1024]{1,0:T(2,128)S(1)}, f32[2,1024]{1,0:T(2,128)}, u32[]{:S(2)}) copy-start(f32[2,1024]{1,0:T(2,128)} %param.15) | copy-start | bytes 24580
  17.7 19.7 %copy-start.12 = (f32[2,1024]{1,0:T(2,128)S(1)}, f32[2,1024]{1,0:T(2,128)}, u32[]{:S(2)}) copy-start(f32[2,1024]{1,0:T(2,128)} %param.16) | copy-start | bytes 24580
  50.2 1.7 copy-start.8
  60.4 1.7 copy-start.2
  104.4 18.2 %copy-start.15 = (u32[32]{0:T(128)S(1)}, u32[32]{0:T(128)}, u32[]{:S(2)}) copy-start(u32[32]{0:T(128)} %constant.44) | copy-start | bytes 388
  104.5 19.4 %copy-start.14 = (s32[12]{0:T(128)S(1)}, s32[12]{0:T(128)}, u32[]{:S(2)}) copy-start(s32[12]{0:T(128)} %param.10) | copy-start | bytes 148
  117.1 28.3 %all-to-all-start = ((bf16[8,2,12,4,512]{4,3,2,1,0:T(4,128)(2,1)}), bf16[8,2,12,4,512]{4,3,2,1,0:T(4,128)(2,1)}, u32[]{:S(2)}, u32[]{:S(2)}) async-start(bf16[8,2,12,4,512]{4,3,2,1,0:T(4,128)(2,1)} %bitcast_dynamic-update-slice_fusion), calls=%async_computation.2 | async-start | bytes 1572864 | tf_op jit(solution)/shard_map/all_to_all | solution.py:97
  147.8 2.2 copy-start.7
  149.9 3.5 %copy-start.4 = (bf16[16,12,4,1024]{3,2,1,0:T(4,128)(2,1)S(1)}, bf16[16,12,4,1024]{3,2,1,0:T(4,128)(2,1)}, u32[]{:S(2)}) copy-start(bf16[16,12,4,1024]{3,2,1,0:T(4,128)(2,1)} %reshape.45) | copy-start | bytes 4718596
  154.6 1.1 copy-start.5
  190.2 15.5 %copy-start.6 = (bf16[16,12,4,1024]{3,2,1,0:T(4,128)(2,1)S(1)}, bf16[16,12,4,1024]{3,2,1,0:T(4,128)(2,1)}, u32[]{:S(2)}) copy-start(bf16[16,12,4,1024]{3,2,1,0:T(4,128)(2,1)} %copy-done.5) | copy-start | bytes 4718596
  205.7 20.4 %copy-start.1 = (bf16[256,1024]{1,0:T(8,128)(2,1)S(1)}, bf16[256,1024]{1,0:T(8,128)(2,1)}, u32[]{:S(2)}) copy-start(bf16[256,1024]{1,0:T(8,128)(2,1)} %param.11) | copy-start | bytes 1572868
  205.7 3.7 %copy-start.13 = (f32[1024]{0:T(1024)S(1)}, f32[1024]{0:T(1024)}, u32[]{:S(2)}) copy-start(f32[1024]{0:T(1024)} %param.17) | copy-start | bytes 12292
Sparse Core Ops, SparseCore 0:
  16.2 33.8 reduce-scatter.2
  104.6 58.2 reduce-scatter.4
Sparse Core Ops, SparseCore 1:
  18.8 46.8 all-gather.1
